TPU v7x, 32 devices: a whole 2x2x4 slice. The times are simulated.
32 devices in a mesh: seq: 16 (over z, y, x), tp: 2 (over core).
Axes of the slice: x: 2, y: 2, z: 4, core: 2. Of those that a mesh axis runs over, the one named last changes fastest.
Arguments:
- tokens: bfloat16 [8192, 2048], P('seq', 'tp'), may hold values from -6 to 6
- ln_gain: bfloat16 [2048], replicated, may hold values from 0.5 to 4.1
- w_qkv: bfloat16 [3, 2048, 2048], P(None, None, 'tp'), may hold values from -0.15467961 to 0.15467961
- w_out: bfloat16 [2048, 2048], P('tp'), may hold values from -0.1875 to 0.1875
Outputs:
- mixed: bfloat16 [8192, 2048], P('seq', 'tp')
All inputs are finite; a program needn't handle non-finite values.
Results may differ from a plain program's by a relative error of at most 0.011.
Values may be sent and summed in bfloat16 or wider, within the bound.
A program may use at most 256 MiB of HBM per device.

v0:
```python
import jax
import jax.numpy as jnp
from jax import lax
from jax.sharding import PartitionSpec as P

HEAD_DIM = 128


def attend_block(totals, queries, block_kv, factor):
    running, denoms, accum = totals
    heads_here = queries.shape[1]
    keys_part = block_kv[0].reshape(block_kv.shape[1], heads_here, queries.shape[2])
    vals_part = block_kv[1].reshape(block_kv.shape[1], heads_here, queries.shape[2])
    scores = (
        jnp.einsum("thc,shc->ths", queries, keys_part, preferred_element_type=jnp.float32) * factor
    )
    highest = jnp.maximum(running, jnp.max(scores, axis=2))
    expon = jnp.exp(scores - highest[:, :, None])
    denoms = jnp.sum(expon, axis=2)
    weights = expon.astype(jnp.bfloat16)
    accum = jnp.einsum("ths,shc->thc", weights, vals_part, preferred_element_type=jnp.float32)
    return (highest, denoms, accum)


def start_totals(rows, heads_count):
    return (
        jnp.full((rows, heads_count), -1e30, jnp.float32),
        jnp.zeros((rows, heads_count), jnp.float32),
        jnp.zeros((rows, heads_count, HEAD_DIM), jnp.float32),
    )


def on_device(tokens, ln_gain, w_qkv, w_out):
    tok_rows = tokens.shape[0]
    whole = lax.all_gather(tokens, "tp", axis=1, tiled=True)
    values = whole.astype(jnp.float32)
    average = jnp.mean(values, axis=1, keepdims=True)
    second = jnp.mean(values * values, axis=1, keepdims=True)
    normed = (
        (values - average)
        * lax.rsqrt(second - average * average + 1e-06)
        * ln_gain.astype(jnp.float32)
    ).astype(jnp.bfloat16)
    projected = jnp.einsum("td,jdc->jtc", normed, w_qkv, preferred_element_type=jnp.float32).astype(
        jnp.bfloat16
    )
    heads_here = w_qkv.shape[2] // HEAD_DIM
    factor = HEAD_DIM ** (-0.5)
    queries = projected[0].reshape(tok_rows, heads_here, HEAD_DIM)
    keys_vals = projected[1:3]
    initial = start_totals(tok_rows, heads_here)
    final = attend_block(
        initial, queries, lax.all_gather(keys_vals, "seq", axis=1, tiled=True), factor
    )
    context = (
        (final[2] / final[1][:, :, None])
        .reshape(tok_rows, heads_here * HEAD_DIM)
        .astype(jnp.bfloat16)
    )
    summed = lax.psum_scatter(
        lax.dot_general(
            w_out, context, (((0,), (1,)), ((), ())), preferred_element_type=jnp.float32
        ).astype(jnp.bfloat16),
        "tp",
        scatter_dimension=0,
        tiled=True,
    ).astype(jnp.float32)
    return (tokens.astype(jnp.float32) + summed.T).astype(jnp.bfloat16)


def solution(mesh):
    in_specs = (P("seq", "tp"), P(), P(None, None, "tp"), P("tp", None))
    out_specs = P("seq", "tp")
    return jax.shard_map(
        on_device, mesh=mesh, in_specs=in_specs, out_specs=out_specs, check_vma=False
    )
```

profile of v0, /device:TPU:0, one launch (start us, length us, event | category | flops | bytes accessed | tf_op | source)
XLA Modules:
  0.0 599.8 jit_solution(8259866064880003707)
XLA Ops:
  6.5 0.0 all-gather.3.cloned.1.call-start
  6.5 0.7 all-gather.3.cloned.1.call-update
  7.3 0.0 all-gather.5.cloned.1.call-start
  7.3 0.7 convert_element_type.39
  8.0 14.2 %all-gather.3.cloned.1.call-done = bf16[512,2048]{1,0:T(8,128)(2,1)} async-done(((bf16[512,1024]{1,0:T(8,128)(2,1)}), bf16[512,2048]{1,0:T(8,128)(2,1)}) %all-gather.3.cloned.1.call-update) | async-done | bytes 2097168 | tf_op jit(solution)/shard_map/all_gather | solution.py:35
  22.2 2.3 convert_reduce_fusion
  24.5 10.5 %convert_bitcast_fusion = bf16[3,512,1024]{2,1,0:T(8,128)(2,1)S(1)} fusion(bf16[3,2048,1024]{2,1,0:T(8,128)(2,1)} %param.6, bf16[512,2048]{1,0:T(8,128)(2,1)} %all-gather.3.cloned.1.call-done, f32[2048]{0:T(1024)S(1)} %convert_element_type.39, f32[512]{0:T(512)S(1)} %get-tuple-element.10, f32[512]{0:T(512)S(1)} %get-tuple-element.9), kind=kOutput, calls=%fused_computation.16 | convolution fusion | flops 6449266688 | bytes 17838080 | tf_op jit(solution)/shard_map/td,jdc->jtc/dot_general | solution.py:44
  35.0 1.5 slice.16
  36.5 0.0 all-gather.5.cloned.1.call-update
  36.5 0.2 reduce-scatter.2.cloned.1.call-start
  36.7 0.1 slice_bitcast_fusion.1
  36.8 0.3 copy.12
  37.1 350.9 %all-gather.5.cloned.1.call-done = bf16[2,8192,1024]{2,1,0:T(8,128)(2,1)} async-done(((bf16[2,512,1024]{2,1,0:T(8,128)(2,1)}), bf16[2,8192,1024]{2,1,0:T(8,128)(2,1)}) %all-gather.5.cloned.1.call-update) | async-done | bytes 33554448 | tf_op jit(solution)/shard_map/all_gather | solution.py:53
  388.0 19.2 %slice_bitcast_fusion = (bf16[1024,8,8,128]{3,1,2,0:T(8,128)(2,1)S(1)}, bf16[1,8192,1024]{2,1,0:T(8,128)(2,1)}) fusion(bf16[2,8192,1024]{2,1,0:T(8,128)(2,1)} %all-gather.5.cloned.1.call-done), kind=kLoop, calls=%fused_computation.6 | loop fusion | bytes 67108864
  407.2 9.1 %copy.11 = bf16[1024,8,8,128]{3,2,1,0:T(8,128)(2,1)} copy(bf16[1024,8,8,128]{3,1,2,0:T(8,128)(2,1)S(1)} %get-tuple-element.7) | data formatting | bytes 33554432
  416.3 20.7 %copy.10 = bf16[1,8192,1024]{1,2,0:T(8,128)(2,1)} copy(bf16[1,8192,1024]{2,1,0:T(8,128)(2,1)} %get-tuple-element.8) | data formatting | bytes 33554432 | tf_op jit(solution)/shard_map/reshape;squeeze | solution.py:13
  437.0 50.1 %bitcast_reduce_fusion = (f32[512,8]{0,1:T(8,128)S(1)}, f32[8,8192,512]{2,1,0:T(8,128)}) fusion(bf16[512,8,128]{2,1,0:T(8,128)(2,1)S(1)} %bitcast.43, bf16[8192,8,128]{2,1,0:T(8,128)(2,1)} %bitcast.41), kind=kOutput, calls=%fused_computation.1 | convolution fusion | flops 8657039360 | bytes 152059904 | tf_op jit(solution)/shard_map/thc,shc->ths/dot_general | solution.py:15
  487.1 41.4 %fusion.1 = f32[512,8]{0,1:T(8,128)S(1)} fusion(f32[8,8192,512]{2,1,0:T(8,128)} %get-tuple-element.12, f32[512,8]{0,1:T(8,128)S(1)} %broadcast_maximum_fusion), kind=kLoop, calls=%fused_computation.3 | loop fusion | flops 100659200 | bytes 134250496 | tf_op jit(solution)/shard_map/reduce_sum | solution.py:19
  528.5 48.2 %fusion.15 = bf16[512,8,128]{0,2,1:T(8,128)(2,1)S(1)} fusion(bf16[8192,8,128]{0,2,1:T(8,128)(2,1)} %bitcast.42, f32[8,8192,512]{2,1,0:T(8,128)} %get-tuple-element.12, f32[512,8]{0,1:T(8,128)S(1)} %broadcast_maximum_fusion, f32[512,8]{0,1:T(8,128)S(1)} %fusion.1), kind=kOutput, calls=%fused_computation.23 | convolution fusion | flops 8691646464 | bytes 152076288 | tf_op jit(solution)/shard_map/ths,shc->thc/dot_general | solution.py:21
  576.7 0.0 copy-start
  576.7 6.0 %fusion.11 = bf16[2048,512]{0,1:T(8,128)(2,1)} fusion(bf16[512,1024]{0,1:T(8,128)(2,1)S(1)} %bitcast.44, bf16[1024,2048]{1,0:T(8,128)(2,1)} %param.7), kind=kOutput, calls=%fused_computation.18 | convolution fusion | flops 2148532224 | bytes 7340032 | tf_op jit(solution)/shard_map/dot_general | solution.py:61
  582.7 0.0 reduce-scatter.2.cloned.1.call-update
  582.8 8.0 %reduce-scatter.2.cloned.1.call-done = bf16[1024,512]{0,1:T(8,128)(2,1)} async-done(((bf16[2048,512]{0,1:T(8,128)(2,1)}), bf16[1024,512]{0,1:T(8,128)(2,1)}) %reduce-scatter.2.cloned.1.call-update) | async-done | bytes 1048592 | tf_op jit(solution)/shard_map/reduce_scatter | solution.py:60
  590.7 0.0 copy-done
  590.7 2.6 fusion.14
  (2 shorter events, 0.0 us)
Async XLA Ops:
  6.5 15.7 %all-gather.3.cloned.1.call-start = ((), (), s32[]{:S(2)}) async-start(), calls=%async_computation.1 | async-start | bytes 3145728 | tf_op jit(solution)/shard_map/all_gather | solution.py:35
  7.3 380.7 %all-gather.5.cloned.1.call-start = ((), (), s32[]{:S(2)}) async-start(), calls=%async_computation.2 | async-start | bytes 35651584 | tf_op jit(solution)/shard_map/all_gather | solution.py:53
  36.5 554.2 %reduce-scatter.2.cloned.1.call-start = ((), (), s32[]{:S(2)}) async-start(), calls=%async_computation.3 | async-start | bytes 3145728 | tf_op jit(solution)/shard_map/reduce_scatter | solution.py:60
  576.7 14.0 %copy-start = (bf16[512,1024]{1,0:T(8,128)(2,1)S(1)}, bf16[512,1024]{1,0:T(8,128)(2,1)}, u32[]{:S(2)}) copy-start(bf16[512,1024]{1,0:T(8,128)(2,1)} %param.4) | copy-start | bytes 3145732
Sparse Core Ops, SparseCore 0:
  8.9 13.2 all-gather.2
  36.6 351.2 all-gather.4
  582.9 7.7 reduce-scatter.1
where the time goes:
time: 601 us; the launch traced here: 600 us
  waiting for transfers between devices  374 us (62%)
  matrix products  115 us (19%)
  local copies, waits for them, and re-layouts  50.9 us (8%)
  other arithmetic  47 us (8%)
  between operations  13.2 us (2%)
    all_gather x1, waiting for transfers between devices, on_device(): lax.all_gather(keys_vals, 'seq', axis=1, tiled=True)  351 us
    dot_general x1, matrix products, attend_block(): jnp.einsum('thc,shc->ths', queries, keys_part, preferred_element_type=jnp...  50.1 us
    dot_general x1, matrix products, attend_block(): jnp.einsum('ths,shc->thc', weights, vals_part, preferred_element_type=jnp...  48.2 us
    reduce_sum x1, other arithmetic, attend_block(): denoms = jnp.sum(expon, axis=2)  41.4 us
    unnamed x6, local copies, waits for them, and re-layouts  28.7 us
    another operation x1, local copies, waits for them, and re-layouts, attend_block(): block_kv[1].reshape(block_kv.shape[1], heads_here, queries.shape[2])  20.7 us
    all_gather x1, waiting for transfers between devices, on_device(): whole = lax.all_gather(tokens, 'tp', axis=1, tiled=True)  14.2 us
  transfers between devices with their start and end apart: 3, of which 3 were waited for; matrix products, arithmetic and copies ran while one was open for 0% of the time, Pallas kernels for 0%

commit v1 on v0

--- a/solution.py
+++ b/solution.py
@@ -2,8 +2,14 @@
 import jax.numpy as jnp
 from jax import lax
 from jax.sharding import PartitionSpec as P
+from jax.lax import all_gather
 
 HEAD_DIM = 128
+
+
+def _fill_rings(u_in):
+    spare = all_gather(u_in, "seq")
+    return jnp.concatenate(spare, 1)
 
 
 def attend_block(totals, queries, block_kv, factor):
@@ -49,9 +55,7 @@
     queries = projected[0].reshape(tok_rows, heads_here, HEAD_DIM)
     keys_vals = projected[1:3]
     initial = start_totals(tok_rows, heads_here)
-    final = attend_block(
-        initial, queries, lax.all_gather(keys_vals, "seq", axis=1, tiled=True), factor
-    )
+    final = attend_block(initial, queries, _fill_rings(keys_vals), factor)
     context = (
         (final[2] / final[1][:, :, None])
         .reshape(tok_rows, heads_here * HEAD_DIM)

time: 601 us -> 606 us (level)
    all_gather x0 -> x1, local copies, waits for them, and re-layouts: none -> 22.6 us  [_fill_rings(): spare = all_gather(u_in, 'seq')]
    another operation x1 -> x0, local copies, waits for them, and re-layouts: 20.7 us -> none  [attend_block(): block_kv[1].reshape(block_kv.shape[1], heads_here, queries.shape[2])]
    slice x0 -> x1, local copies, waits for them, and re-layouts: none -> 12.7 us  [attend_block(): block_kv[1].reshape(block_kv.shape[1], heads_here, queries.shape[2])]
    unnamed x6, local copies, waits for them, and re-layouts: 28.7 us -> 18.6 us
where the time goes in v1:
time: 606 us; the launch traced here: 605 us
  waiting for transfers between devices  374 us (62%)
  matrix products  116 us (19%)
  local copies, waits for them, and re-layouts  55.4 us (9%)
  other arithmetic  47 us (8%)
  between operations  13.2 us (2%)
    all_gather x1, waiting for transfers between devices, _fill_rings(): spare = all_gather(u_in, 'seq')  351 us
    dot_general x1, matrix products, attend_block(): jnp.einsum('thc,shc->ths', queries, keys_part, preferred_element_type=jnp...  50 us
    dot_general x1, matrix products, attend_block(): jnp.einsum('ths,shc->thc', weights, vals_part, preferred_element_type=jnp...  49.1 us
    reduce_sum x1, other arithmetic, attend_block(): denoms = jnp.sum(expon, axis=2)  41.4 us
    all_gather x1, local copies, waits for them, and re-layouts, _fill_rings(): spare = all_gather(u_in, 'seq')  22.6 us
    unnamed x6, local copies, waits for them, and re-layouts  18.6 us
    all_gather x1, waiting for transfers between devices, on_device(): whole = lax.all_gather(tokens, 'tp', axis=1, tiled=True)  14.2 us
    slice x1, local copies, waits for them, and re-layouts, attend_block(): block_kv[1].reshape(block_kv.shape[1], heads_here, queries.shape[2])  12.7 us
  transfers between devices with their start and end apart: 3, of which 3 were waited for; matrix products, arithmetic and copies ran while one was open for 0% of the time, Pallas kernels for 0%

profile of v1, /device:TPU:0, one launch (start us, length us, event | category | flops | bytes accessed | tf_op | source)
XLA Modules:
  0.0 605.3 jit_solution(3589919115182919512)
XLA Ops:
  6.5 0.0 all-gather.4.cloned.1.call-start
  6.5 0.7 all-gather.4.cloned.1.call-update
  7.3 0.0 all-gather.6.cloned.1.call-start
  7.3 0.7 convert_element_type.39
  8.0 14.2 %all-gather.4.cloned.1.call-done = bf16[512,2048]{1,0:T(8,128)(2,1)} async-done(((bf16[512,1024]{1,0:T(8,128)(2,1)}), bf16[512,2048]{1,0:T(8,128)(2,1)}) %all-gather.4.cloned.1.call-update) | async-done | bytes 2097168 | tf_op jit(solution)/shard_map/all_gather | solution.py:41
  22.2 2.3 convert_reduce_fusion
  24.5 10.5 %convert_bitcast_fusion = bf16[3,512,1024]{2,1,0:T(8,128)(2,1)S(1)} fusion(bf16[3,2048,1024]{2,1,0:T(8,128)(2,1)} %param.6, bf16[512,2048]{1,0:T(8,128)(2,1)} %all-gather.4.cloned.1.call-done, f32[2048]{0:T(1024)S(1)} %convert_element_type.39, f32[512]{0:T(512)S(1)} %get-tuple-element.10, f32[512]{0:T(512)S(1)} %get-tuple-element.9), kind=kOutput, calls=%fused_computation.17 | convolution fusion | flops 6449266688 | bytes 17838080 | tf_op jit(solution)/shard_map/td,jdc->jtc/dot_general | solution.py:50
  35.0 1.5 slice.18
  36.5 0.0 all-gather.6.cloned.1.call-update
  36.5 0.2 reduce-scatter.2.cloned.1.call-start
  36.7 0.1 slice_bitcast_fusion
  36.8 0.3 copy.22
  37.1 351.0 %all-gather.6.cloned.1.call-done = bf16[32,512,1024]{2,1,0:T(8,128)(2,1)} async-done(((bf16[2,512,1024]{2,1,0:T(8,128)(2,1)}), bf16[32,512,1024]{2,1,0:T(8,128)(2,1)}) %all-gather.6.cloned.1.call-update) | async-done | bytes 33554448 | tf_op jit(solution)/shard_map/all_gather | solution.py:11
  388.1 22.6 %copy.36 = bf16[16,2,512,1024]{3,2,0,1:T(8,128)(2,1)} copy(bf16[16,2,512,1024]{3,2,1,0:T(8,128)(2,1)} %bitcast.51) | data formatting | bytes 67108864 | tf_op jit(solution)/shard_map/all_gather | solution.py:11
  410.7 12.7 %fusion.26 = (bf16[1,16,512,1024]{3,2,1,0:T(8,128)(2,1)S(1)}, bf16[1,16,512,1024]{3,2,1,0:T(8,128)(2,1)S(1)}) fusion(bf16[2,16,512,1024]{3,2,1,0:T(8,128)(2,1)} %bitcast.47), kind=kLoop, calls=%fused_computation.34 | loop fusion | bytes 67108864 | tf_op jit(solution)/shard_map/slice | solution.py:19
  423.4 9.1 %copy.20 = bf16[1024,8,8,128]{3,2,1,0:T(8,128)(2,1)} copy(bf16[1024,8,8,128]{3,1,2,0:T(8,128)(2,1)S(1)} %bitcast.50) | data formatting | bytes 33554432
  432.5 9.1 %copy.21 = bf16[1024,8,8,128]{3,2,1,0:T(8,128)(2,1)} copy(bf16[1024,8,8,128]{3,1,2,0:T(8,128)(2,1)S(1)} %bitcast.49) | data formatting | bytes 33554432
  441.6 50.0 %bitcast_reduce_fusion = (f32[512,8]{0,1:T(8,128)S(1)}, f32[8,8192,512]{2,1,0:T(8,128)}) fusion(bf16[512,8,128]{2,1,0:T(8,128)(2,1)S(1)} %bitcast.53, bf16[8192,8,128]{2,1,0:T(8,128)(2,1)} %bitcast.48), kind=kOutput, calls=%fused_computation.1 | convolution fusion | flops 8657039360 | bytes 152059904 | tf_op jit(solution)/shard_map/thc,shc->ths/dot_general | solution.py:21
  491.7 41.4 %fusion.1 = f32[512,8]{0,1:T(8,128)S(1)} fusion(f32[8,8192,512]{2,1,0:T(8,128)} %get-tuple-element.12, f32[512,8]{0,1:T(8,128)S(1)} %broadcast_maximum_fusion), kind=kLoop, calls=%fused_computation.3 | loop fusion | flops 100659200 | bytes 134250496 | tf_op jit(solution)/shard_map/reduce_sum | solution.py:25
  533.1 49.1 %fusion.16 = bf16[512,8,128]{0,2,1:T(8,128)(2,1)S(1)} fusion(f32[8,8192,512]{2,1,0:T(8,128)} %get-tuple-element.12, f32[512,8]{0,1:T(8,128)S(1)} %broadcast_maximum_fusion, bf16[8192,8,128]{2,1,0:T(8,128)(2,1)} %bitcast.52, f32[512,8]{0,1:T(8,128)S(1)} %fusion.1), kind=kOutput, calls=%fused_computation.24 | convolution fusion | flops 8691646464 | bytes 152076288 | tf_op jit(solution)/shard_map/ths,shc->thc/dot_general | solution.py:27
  582.2 0.0 copy-start
  582.2 6.0 fusion.12
  588.2 0.0 reduce-scatter.2.cloned.1.call-update
  588.3 8.0 %reduce-scatter.2.cloned.1.call-done = bf16[1024,512]{0,1:T(8,128)(2,1)} async-done(((bf16[2048,512]{0,1:T(8,128)(2,1)}), bf16[1024,512]{0,1:T(8,128)(2,1)}) %reduce-scatter.2.cloned.1.call-update) | async-done | bytes 1048592 | tf_op jit(solution)/shard_map/reduce_scatter | solution.py:64
  596.2 0.0 copy-done
  596.2 2.6 fusion.15
  (2 shorter events, 0.0 us)
Async XLA Ops:
  6.5 15.7 %all-gather.4.cloned.1.call-start = ((), (), s32[]{:S(2)}) async-start(), calls=%async_computation.1 | async-start | bytes 3145728 | tf_op jit(solution)/shard_map/all_gather | solution.py:41
  7.3 380.8 %all-gather.6.cloned.1.call-start = ((), (), s32[]{:S(2)}) async-start(), calls=%async_computation.3 | async-start | bytes 35651584 | tf_op jit(solution)/shard_map/all_gather | solution.py:11
  36.5 559.7 %reduce-scatter.2.cloned.1.call-start = ((), (), s32[]{:S(2)}) async-start(), calls=%async_computation.2 | async-start | bytes 3145728 | tf_op jit(solution)/shard_map/reduce_scatter | solution.py:64
  582.2 14.0 %copy-start = (bf16[512,1024]{1,0:T(8,128)(2,1)S(1)}, bf16[512,1024]{1,0:T(8,128)(2,1)}, u32[]{:S(2)}) copy-start(bf16[512,1024]{1,0:T(8,128)(2,1)} %param.4) | copy-start | bytes 3145732
Sparse Core Ops, SparseCore 0:
  8.9 13.2 all-gather.3
  36.6 351.4 all-gather.5
  588.4 7.7 reduce-scatter.1
